TPU v7x, 32 devices: a whole 2x2x4 slice. The times are simulated.
32 devices in a mesh: seq: 8 (over y, x, core), wshard: 4 (over z).
Axes of the slice: x: 2, y: 2, z: 4, core: 2. Of those that a mesh axis runs over, the one named last changes fastest.
Arguments:
- block_in: bfloat16 [4, 2048, 1536], P('wshard', 'seq'), may hold values from -6 to 6
- cotangent: bfloat16 [4, 2048, 1536], P('wshard', 'seq'), may hold values from -6 to 6
- in_weight: float32 [1536, 6448], P(('seq', 'wshard')), may hold values from -0.15625 to 0.15625
- out_weight: float32 [3072, 1536], P(('seq', 'wshard')), may hold values from -0.109375 to 0.109375
- in_gain: float32 [1536], replicated, may hold values from 0.5 to 1.5
- out_gain: float32 [3072], replicated, may hold values from 0.5 to 1.5
- conv_inner: float32 [5, 3072], replicated, may hold values from -3 to 3
- conv_shared: float32 [5, 256], replicated, may hold values from -3 to 3
- head_params: float32 [3, 48], replicated, may hold values from -5 to 1.5, as said below
- first_in_weight: float32 [1536, 6448], P(('seq', 'wshard')), may hold values from -6 to 6
- first_out_weight: float32 [3072, 1536], P(('seq', 'wshard')), may hold values from -6 to 6
- first_in_gain: float32 [1536], replicated, may hold values from -6 to 6
- first_out_gain: float32 [3072], replicated, may hold values from -6 to 6
- first_conv_inner: float32 [5, 3072], replicated, may hold values from -6 to 6
- first_conv_shared: float32 [5, 256], replicated, may hold values from -6 to 6
- first_head_params: float32 [3, 48], replicated, may hold values from -6 to 6
- second_in_weight: float32 [1536, 6448], P(('seq', 'wshard')), may hold values from 0.01 to 1
- second_out_weight: float32 [3072, 1536], P(('seq', 'wshard')), may hold values from 0.01 to 1
- second_in_gain: float32 [1536], replicated, may hold values from 16.384 to 1638.4
- second_out_gain: float32 [3072], replicated, may hold values from 0.01 to 1
- second_conv_inner: float32 [5, 3072], replicated, may hold values from 0.01 to 1
- second_conv_shared: float32 [5, 256], replicated, may hold values from 0.01 to 1
- second_head_params: float32 [3, 48], replicated, may hold values from 0.01 to 1
Outputs:
- block_out: float32 [4, 2048, 1536], P('wshard', 'seq')
- grad_in: float32 [4, 2048, 1536], P('wshard', 'seq')
- grad_in_weight: float32 [1536, 6448], P(('seq', 'wshard'))
- grad_out_weight: float32 [3072, 1536], P(('seq', 'wshard'))
- grad_in_gain: float32 [1536], replicated
- grad_out_gain: float32 [3072], replicated
- grad_conv_inner: float32 [5, 3072], replicated
- grad_conv_shared: float32 [5, 256], replicated
- grad_head_params: float32 [3, 48], replicated
- new_in_weight: float32 [1536, 6448], P(('seq', 'wshard'))
- new_out_weight: float32 [3072, 1536], P(('seq', 'wshard'))
- updated_input_gain: float32 [1536], replicated
- new_out_gain: float32 [3072], replicated
- new_conv_inner: float32 [5, 3072], replicated
- new_conv_shared: float32 [5, 256], replicated
- new_head_params: float32 [3, 48], replicated
- new_first_in_weight: float32 [1536, 6448], P(('seq', 'wshard'))
- new_first_out_weight: float32 [3072, 1536], P(('seq', 'wshard'))
- new_first_in_gain: float32 [1536], replicated
- new_first_out_gain: float32 [3072], replicated
- new_first_conv_inner: float32 [5, 3072], replicated
- new_first_conv_shared: float32 [5, 256], replicated
- updated_head_first_moment: float32 [3, 48], replicated
- new_second_in_weight: float32 [1536, 6448], P(('seq', 'wshard'))
- new_second_out_weight: float32 [3072, 1536], P(('seq', 'wshard'))
- new_second_in_gain: float32 [1536], replicated
- new_second_out_gain: float32 [3072], replicated
- new_second_conv_inner: float32 [5, 3072], replicated
- new_second_conv_shared: float32 [5, 256], replicated
- new_second_head_params: float32 [2, 48], replicated
- new_second_skip: float32 [48], replicated
Inputs may be any that keep to these rules, and one draw needn't show every extreme that they name: `head_params`: row 0 holds step biases, row 1 logarithms of decay rates, row 2 skip gains.
All inputs are finite; a program needn't handle non-finite values.
Results may differ from a plain program's by a relative error of at most 0.02.
The roundings to bfloat16 on the way count: a program that leaves them out, or rounds other values in their place, can miss the bound.
Values may be sent and summed in bfloat16 or wider, within the bound.
A program may use at most 256 MiB of HBM per device.

v0:
```python
import jax
import jax.numpy as jnp
from jax import lax
from jax.sharding import PartitionSpec as P

P_SIZE = 64
N_STATE = 128
BLOCK_LEN = 256
E = 3072
norm_eps = 1e-05
beta_one = 0.9
beta_two = 0.95
adam_eps = 1e-08
adam_step = 3.0
weight_learning_rate = 0.01
matrix_decay = 0.1
small_rate = 0.1


def causal_conv(values, taps):
    length = values.shape[1]
    width = taps.shape[0] - 1
    padded = jnp.pad(values, ((0, 0), (width - 1, 0), (0, 0)))
    total = taps[width] + taps[0] * padded[:, 0:length]
    for shift in range(1, width):
        total = total + taps[shift] * padded[:, shift : shift + length]
    return total


def block_step(state, inputs):
    inner_part, step_part, learning_rate_piece, b_part, c_part = inputs
    high = lax.Precision.HIGHEST
    cumul = jnp.cumsum(learning_rate_piece, axis=1)
    scores = jnp.einsum("sin,sjn->sij", c_part, b_part, precision=high)
    rows = lax.broadcasted_iota(jnp.int32, (BLOCK_LEN, BLOCK_LEN), 0)
    cols = lax.broadcasted_iota(jnp.int32, (BLOCK_LEN, BLOCK_LEN), 1)
    lower = (rows >= cols)[None, :, :, None]
    spread = cumul[:, :, None, :] - cumul[:, None, :, :]
    decay = jnp.where(lower, jnp.exp(jnp.where(lower, spread, 0.0)), 0.0)
    weights = scores[..., None] * decay * step_part[:, None, :, :]
    within = jnp.einsum("sijh,sjhp->sihp", weights, inner_part, precision=high)
    carried = (
        jnp.einsum("sin,shpn->sihp", c_part, state, precision=high) * jnp.exp(cumul)[..., None]
    )
    tail = jnp.exp(cumul[:, -1:, :] - cumul) * step_part
    fresh = jnp.einsum("sjn,sjh,sjhp->shpn", b_part, tail, inner_part, precision=high)
    new_state = jnp.exp(cumul[:, -1, :])[:, :, None, None] * state + fresh
    return (new_state, within + carried)


def state_space(inner, step, rate, b_mat, c_mat):
    batch, length, heads, head_size = inner.shape
    blocks = length // BLOCK_LEN

    def blockify(values):
        return jnp.moveaxis(values.reshape((batch, blocks, BLOCK_LEN) + values.shape[2:]), 1, 0)

    start = jnp.zeros((batch, heads, head_size, b_mat.shape[2]), dtype=inner.dtype)
    _, outputs = lax.scan(
        jax.checkpoint(block_step),
        start,
        (blockify(inner), blockify(step), blockify(rate), blockify(b_mat), blockify(c_mat)),
    )
    return jnp.moveaxis(outputs, 0, 1).reshape(batch, length, heads, head_size)


def mixer(gate_inner, shared, step_raw, conv_local, conv_common, head_local):
    batch, length = (gate_inner.shape[0], gate_inner.shape[1])
    heads = step_raw.shape[2]
    parts = gate_inner.reshape(batch, length, heads, 2, P_SIZE)
    gate_vals = parts[:, :, :, 0, :].reshape(batch, length, heads * P_SIZE)
    inner_vals = parts[:, :, :, 1, :].reshape(batch, length, heads * P_SIZE)
    inner_act = jax.nn.silu(causal_conv(inner_vals, conv_local))
    shared_act = jax.nn.silu(causal_conv(shared, conv_common))
    half = shared.shape[2] // 2
    step = jax.nn.softplus(step_raw + head_local[0])
    rate = -step * jnp.exp(head_local[1])
    inner_heads = inner_act.reshape(batch, length, heads, P_SIZE)
    output = state_space(inner_heads, step, rate, shared_act[..., :half], shared_act[..., half:])
    output = output + head_local[2][:, None] * inner_heads
    return output.reshape(batch, length, heads * P_SIZE) * jax.nn.silu(gate_vals)


def adamw(param, grad, first, second_moment, rate, decay):
    first_new = beta_one * first + (1.0 - beta_one) * grad
    second_new = beta_two * second_moment + (1.0 - beta_two) * grad * grad
    corrected = (
        first_new
        / (1.0 - beta_one**adam_step)
        / (jnp.sqrt(second_new / (1.0 - beta_two**adam_step)) + adam_eps)
    )
    return (param - rate * (corrected + decay * param), first_new, second_new)


def local(
    block_in,
    cotangent,
    in_weight,
    out_weight,
    in_gain,
    out_gain,
    conv_inner,
    conv_shared,
    head_params,
    first_in_weight,
    first_out_weight,
    first_in_gain,
    first_out_gain,
    first_conv_inner,
    first_conv_shared,
    first_head_params,
    second_in_weight,
    second_out_weight,
    second_in_gain,
    second_out_gain,
    second_conv_inner,
    second_conv_shared,
    second_head_params,
):
    seq_index = lax.axis_index("seq")
    inputs = block_in.astype(jnp.float32)
    rms_in = lax.rsqrt(jnp.mean(inputs * inputs, axis=-1, keepdims=True) + norm_eps)
    normed = (inputs * rms_in * in_gain).astype(jnp.bfloat16)
    in_w16 = in_weight.astype(jnp.bfloat16)
    out_w16 = out_weight.astype(jnp.bfloat16)
    column_list = normed
    projected = jnp.einsum(
        "fbe,ek->fbk",
        column_list,
        lax.all_gather(in_w16, ("seq", "wshard"), axis=0, tiled=True),
        preferred_element_type=jnp.float32,
    ).astype(jnp.bfloat16)
    gate_inner = projected[:, :, : 2 * E]
    shared = projected[:, :, 2 * E : 2 * E + 2 * N_STATE]
    step_raw = projected[:, :, 2 * E + 2 * N_STATE :]
    head_gate, head_step = (
        lax.all_to_all(gate_inner, "seq", split_axis=2, concat_axis=1, tiled=True),
        lax.all_to_all(step_raw, "seq", split_axis=2, concat_axis=1, tiled=True),
    )
    head_shared = lax.all_gather(shared, "seq", axis=1, tiled=True)
    heads_dev = head_step.shape[2]
    inner_start = seq_index * (heads_dev * P_SIZE)
    conv_local = lax.dynamic_slice_in_dim(conv_inner, inner_start, heads_dev * P_SIZE, 1)
    head_local = lax.dynamic_slice_in_dim(head_params, seq_index * heads_dev, heads_dev, 1)
    gated, mixer_back = jax.vjp(
        mixer,
        head_gate.astype(jnp.float32),
        head_shared.astype(jnp.float32),
        head_step.astype(jnp.float32),
        conv_local,
        conv_shared,
        head_local,
    )
    gated32 = lax.all_to_all(
        gated.astype(jnp.bfloat16), "seq", split_axis=1, concat_axis=2, tiled=True
    ).astype(jnp.float32)
    rms_out = lax.rsqrt(jnp.mean(gated32 * gated32, axis=-1, keepdims=True) + norm_eps)
    gnormed = (gated32 * rms_out * out_gain).astype(jnp.bfloat16)
    column_list = gnormed
    mixed = jnp.einsum(
        "brg,ga->bra",
        column_list,
        lax.all_gather(out_w16, ("seq", "wshard"), axis=0, tiled=True),
        preferred_element_type=jnp.float32,
    )
    d_gnormed = jnp.einsum(
        "oum,am->oua",
        cotangent,
        lax.all_gather(out_w16, ("seq", "wshard"), axis=0, tiled=True),
        preferred_element_type=jnp.float32,
    )
    block_out = inputs + mixed
    d_out_gain = jnp.sum(d_gnormed * gated32 * rms_out, axis=(0, 1))
    scaled = d_gnormed * out_gain
    d_gated = (
        rms_out * scaled - gated32 * rms_out**3 * jnp.mean(scaled * gated32, axis=-1, keepdims=True)
    ).astype(jnp.bfloat16)
    head_cotan = lax.all_to_all(d_gated, "seq", split_axis=2, concat_axis=1, tiled=True).astype(
        jnp.float32
    )
    d_gate, d_shared, d_step, d_conv_local, d_common, d_head_local = mixer_back(head_cotan)
    tok_gate, tok_step = (
        lax.all_to_all(d_gate.astype(jnp.bfloat16), "seq", split_axis=1, concat_axis=2, tiled=True),
        lax.all_to_all(d_step.astype(jnp.bfloat16), "seq", split_axis=1, concat_axis=2, tiled=True),
    )
    shared_sum = lax.psum_scatter(
        d_shared.astype(jnp.bfloat16), "seq", scatter_dimension=1, tiled=True
    )
    projected_gradient = jnp.concatenate([tok_gate, shared_sum, tok_step], axis=2)
    d_normed = jnp.einsum(
        "ozu,hu->ozh",
        projected_gradient,
        lax.all_gather(in_w16, ("seq", "wshard"), axis=0, tiled=True),
        preferred_element_type=jnp.float32,
    )
    d_in_gain = jnp.sum(d_normed * inputs * rms_in, axis=(0, 1))
    scaled_in = d_normed * in_gain
    grad_in = (
        cotangent.astype(jnp.float32)
        + rms_in * scaled_in
        - inputs * rms_in**3 * jnp.mean(scaled_in * inputs, axis=-1, keepdims=True)
    )
    d_conv_full = lax.dynamic_update_slice_in_dim(
        jnp.zeros_like(conv_inner), d_conv_local, inner_start, 1
    )
    d_head_full = lax.dynamic_update_slice_in_dim(
        jnp.zeros_like(head_params), d_head_local, seq_index * heads_dev, 1
    )
    grad_in_gain, grad_out_gain, grad_conv_inner, grad_conv_shared, grad_head_params = lax.psum(
        (d_in_gain, d_out_gain, d_conv_full, d_common, d_head_full), ("seq", "wshard")
    )
    column_list = normed
    grad_in_weight = lax.psum_scatter(
        jnp.einsum(
            "nkm,nkc->mc", column_list, projected_gradient, preferred_element_type=jnp.float32
        ),
        ("seq", "wshard"),
        scatter_dimension=0,
        tiled=True,
    )
    column_list = gnormed
    grad_out_weight = lax.psum_scatter(
        jnp.einsum("kcb,kch->bh", column_list, cotangent, preferred_element_type=jnp.float32),
        ("seq", "wshard"),
        scatter_dimension=0,
        tiled=True,
    )
    new_in_weight, new_first_in_weight, new_second_in_weight = adamw(
        in_weight,
        grad_in_weight,
        first_in_weight,
        second_in_weight,
        weight_learning_rate,
        matrix_decay,
    )
    new_out_weight, new_first_out_weight, new_second_out_weight = adamw(
        out_weight,
        grad_out_weight,
        first_out_weight,
        second_out_weight,
        weight_learning_rate,
        matrix_decay,
    )
    updated_input_gain, new_first_in_gain, new_second_in_gain = adamw(
        in_gain, grad_in_gain, first_in_gain, second_in_gain, small_rate, 0.0
    )
    new_out_gain, new_first_out_gain, new_second_out_gain = adamw(
        out_gain, grad_out_gain, first_out_gain, second_out_gain, small_rate, 0.0
    )
    new_conv_inner, new_first_conv_inner, new_second_conv_inner = adamw(
        conv_inner, grad_conv_inner, first_conv_inner, second_conv_inner, small_rate, 0.0
    )
    new_conv_shared, new_first_conv_shared, new_second_conv_shared = adamw(
        conv_shared, grad_conv_shared, first_conv_shared, second_conv_shared, small_rate, 0.0
    )
    new_head_params, updated_head_first_moment, head_second_all = adamw(
        head_params, grad_head_params, first_head_params, second_head_params, small_rate, 0.0
    )
    return (
        block_out,
        grad_in,
        grad_in_weight,
        grad_out_weight,
        grad_in_gain,
        grad_out_gain,
        grad_conv_inner,
        grad_conv_shared,
        grad_head_params,
        new_in_weight,
        new_out_weight,
        updated_input_gain,
        new_out_gain,
        new_conv_inner,
        new_conv_shared,
        new_head_params,
        new_first_in_weight,
        new_first_out_weight,
        new_first_in_gain,
        new_first_out_gain,
        new_first_conv_inner,
        new_first_conv_shared,
        updated_head_first_moment,
        new_second_in_weight,
        new_second_out_weight,
        new_second_in_gain,
        new_second_out_gain,
        new_second_conv_inner,
        new_second_conv_shared,
        head_second_all[0:2],
        head_second_all[2],
    )


def solution(mesh):
    return jax.shard_map(
        local,
        mesh=mesh,
        in_specs=(
            P("wshard", "seq", None),
            P("wshard", "seq", None),
            P(("seq", "wshard"), None),
            P(("seq", "wshard"), None),
            P(),
            P(),
            P(),
            P(),
            P(),
            P(("seq", "wshard"), None),
            P(("seq", "wshard"), None),
            P(),
            P(),
            P(),
            P(),
            P(),
            P(("seq", "wshard"), None),
            P(("seq", "wshard"), None),
            P(),
            P(),
            P(),
            P(),
            P(),
        ),
        out_specs=(
            P("wshard", "seq", None),
            P("wshard", "seq", None),
            P(("seq", "wshard"), None),
            P(("seq", "wshard"), None),
            P(),
            P(),
            P(),
            P(),
            P(),
            P(("seq", "wshard"), None),
            P(("seq", "wshard"), None),
            P(),
            P(),
            P(),
            P(),
            P(),
            P(("seq", "wshard"), None),
            P(("seq", "wshard"), None),
            P(),
            P(),
            P(),
            P(),
            P(),
            P(("seq", "wshard"), None),
            P(("seq", "wshard"), None),
            P(),
            P(),
            P(),
            P(),
            P(),
            P(),
        ),
        check_vma=False,
    )
```

profile of v0, /device:TPU:0, one launch (start us, length us, event | category | flops | bytes accessed | tf_op | source)
XLA Modules:
  0.0 2023.6 jit_solution(13329375079531035761)
XLA Ops:
  11.6 132.1 %all-gather.4.cloned.1.call-done = bf16[1536,6448]{1,0:T(8,128)(2,1)} async-done(((bf16[48,6448]{1,0:T(8,128)(2,1)}), bf16[1536,6448]{1,0:T(8,128)(2,1)}) %all-gather.4.cloned.1.call-update) | async-done | bytes 19808272 | tf_op jit(solution)/shard_map/all_gather | solution.py:130
  143.6 14.0 fusion.107
  167.6 37.2 %copy.613 = bf16[1,256,6144]{1,0,2:T(2,128)(2,1)} copy(bf16[1,256,6144]{1,2,0:T(8,128)(2,1)S(1)} %slice.200) | data formatting | bytes 6291456 | tf_op jit(solution)/shard_map/slice | solution.py:133
  204.9 31.5 %reduce.89 = bf16[6144,256]{1,0:T(8,128)(2,1)S(1)} reduce(bf16[6144,1,256]{2,1,0:T(2,128)(2,1)} %bitcast.657, bf16[]{:T(256)} %broadcast.1020), dimensions={1}, to_apply=%bitcast.470.reduce_sub_computation | reduce | bytes 6291458
  259.4 23.1 %all-to-all-done.1 = bf16[8,2,98304]{2,1,0:T(2,128)(2,1)S(1)} async-done(((bf16[8,2,98304]{2,1,0:T(2,128)(2,1)}), bf16[8,2,98304]{2,1,0:T(2,128)(2,1)S(1)}, u32[]{:S(2)}, u32[]{:S(2)}) %all-to-all-start.1) | async-done | bytes 3145760 | tf_op jit(solution)/shard_map/all_to_all | solution.py:137
  317.7 185.0 %while.44 = (s32[]{:T(128)}, f32[1,6,64,128]{3,2,1,0:T(8,128)S(1)}, f32[8,1,256,6,64]{2,0,4,3,1:T(8,128)}, f32[8,1,6,64,128]{4,3,2,1,0:T(8,128)}, f32[8,1,256,6]...) while((s32[]{:T(128)}, f32[1,6,64,128]{3,2,1,0:T(8,128)S(1)}, ...), condition=%wide.region_4.5_spmd.clone.clone, body=%wide.region_1.4_spmd.clone.clone.sunk | while | flops 707349504 | bytes 5805416 | solution.py:59
  331.4 9.8 dynamic_update_slice.95
  520.5 35.5 %reduce.90 = bf16[2048,384]{1,0:T(8,128)(2,1)} reduce(bf16[2048,1,384]{2,1,0:T(2,128)(2,1)} %bitcast.669, bf16[]{:T(256)} %broadcast.1020), dimensions={1}, to_apply=%bitcast.432.reduce_sub_computation | reduce | bytes 3145730
  564.1 20.9 %all-to-all-done.2 = bf16[8,2,49152]{2,1,0:T(2,128)(2,1)} async-done(((bf16[8,2,49152]{2,1,0:T(2,128)(2,1)}), bf16[8,2,49152]{2,1,0:T(2,128)(2,1)}, u32[]{:S(2)}, u32[]{:S(2)}) %all-to-all-start.2) | async-done | bytes 1572896 | tf_op jit(solution)/shard_map/all_to_all | solution.py:154
  600.2 10.7 fusion.139
  610.9 204.3 %reduce-scatter.8.cloned.1.call-done = f32[96,1536]{1,0:T(8,128)} async-done(((f32[3072,1536]{1,0:T(8,128)}), f32[96,1536]{1,0:T(8,128)}) %reduce-scatter.8.cloned.1.call-update) | async-done | bytes 589840 | tf_op jit(solution)/shard_map/reduce_scatter | solution.py:222
  822.5 76.8 %all-gather.8.cloned.1.call-done = bf16[3072,1536]{1,0:T(8,128)(2,1)} async-done(((bf16[96,1536]{1,0:T(8,128)(2,1)}), bf16[3072,1536]{1,0:T(8,128)(2,1)}) %all-gather.8.cloned.1.call-update) | async-done | bytes 9437200 | tf_op jit(solution)/shard_map/all_gather | solution.py:163
  917.6 17.8 reduce.91
  947.2 17.2 all-to-all-done.3
  981.4 355.6 %while.43 = (s32[]{:T(128)}, f32[1,6,64,128]{3,2,1,0:T(8,128)S(1)}, f32[8,1,256,6,64]{2,0,4,3,1:T(8,128)}, f32[8,1,256,6]{3,2,1,0:T(8,128)}, f32[8,1,256,6]{2,0,...) while((s32[]{:T(128)}, f32[1,6,64,128]{3,2,1,0:T(8,128)S(1)}, ...), condition=%wide.region_19.20_spmd.clone, body=%wide.region_7.19_spmd.clone.sunk | while | flops 1670419456 | bytes 15714059 | solution.py:59
  1341.8 11.5 reduce.92
  1369.0 12.4 multiply_reduce_fusion.6
  1392.1 15.7 copy.509
  1407.8 31.6 %reduce.93 = bf16[2048,768]{1,0:T(8,128)(2,1)S(1)} reduce(bf16[2048,1,768]{2,1,0:T(2,128)(2,1)} %bitcast.656, bf16[]{:T(256)} %broadcast.1020), dimensions={1}, to_apply=%bitcast.438.reduce_sub_computation | reduce | bytes 6291458
  1460.7 27.7 %all-to-all-done.4 = bf16[8,2,98304]{2,1,0:T(2,128)(2,1)} async-done(((bf16[8,2,98304]{2,1,0:T(2,128)(2,1)}), bf16[8,2,98304]{2,1,0:T(2,128)(2,1)}, u32[]{:S(2)}, u32[]{:S(2)}) %all-to-all-start.4) | async-done | bytes 3145760 | tf_op jit(solution)/shard_map/all_to_all | solution.py:183
  1502.4 12.5 fusion.132
  1515.0 18.5 fusion.135
  1545.1 94.3 %all-reduce.32.cloned.1.call-done = (f32[1536]{0:T(1024)}, f32[3072]{0:T(1024)}, f32[5,3072]{1,0:T(8,128)}, f32[5,256]{1,0:T(8,128)}, f32[3,48]{1,0:T(4,128)}) async-done(((f32[1536]{0:T(1024)}, f32[3072]{0:T(1024)}, f32[5,3072]{1,0:T(8,128)}, f32[5,256]{1,0:T(8,128)}, f32[3,48]{1,0:T(4,128)}), (f32[1536]{0:T(1024)}, f32[3072]{0:T(1024)}, f32[5,3072]{1,0:T(8,128)}, f32[5,256]{1,0:T(8,128)}, ...) | async-done | bytes 85584 | tf_op jit(solution)/shard_map/psum | solution.py:209
  1647.4 361.7 %reduce-scatter.6.cloned.1.call-done = f32[48,6448]{1,0:T(8,128)} async-done(((f32[1536,6448]{1,0:T(8,128)}), f32[48,6448]{1,0:T(8,128)}) %reduce-scatter.6.cloned.1.call-update) | async-done | bytes 1238032 | tf_op jit(solution)/shard_map/reduce_scatter | solution.py:213
  (963 shorter events, 787.9 us)
Async XLA Ops:
  7.2 136.4 %all-gather.4.cloned.1.call-start = ((), (), s32[]{:S(2)}) async-start(), calls=%async_computation.9 | async-start | bytes 20680704 | tf_op jit(solution)/shard_map/all_gather | solution.py:130
  9.6 238.6 %all-gather.6.cloned.1.call-start = ((), (), s32[]{:S(2)}) async-start(), calls=%async_computation.10 | async-start | bytes 1179648 | tf_op jit(solution)/shard_map/all_gather | solution.py:140
  11.6 146.1 %copy-start.48 = (f32[256]{0:T(256)}, f32[256]{0:T(256)S(1)}, u32[]{:S(2)}) copy-start(f32[256]{0:T(256)S(1)} %get-tuple-element.934) | copy-start | bytes 3076
  162.0 78.0 %all-to-all-start = ((bf16[8,2,768]{2,1,0:T(2,128)(2,1)}), bf16[8,2,768]{2,1,0:T(2,128)(2,1)S(1)}, u32[]{:S(2)}, u32[]{:S(2)}) async-start(bf16[8,2,768]{2,1,0:T(2,128)(2,1)} %reshape.1691), calls=%async_computation | async-start | bytes 49152 | tf_op jit(solution)/shard_map/all_to_all | solution.py:138
  240.0 42.4 %all-to-all-start.1 = ((bf16[8,2,98304]{2,1,0:T(2,128)(2,1)}), bf16[8,2,98304]{2,1,0:T(2,128)(2,1)S(1)}, u32[]{:S(2)}, u32[]{:S(2)}) async-start(bf16[8,2,98304]{2,1,0:T(2,128)(2,1)} %reshape.1693), calls=%async_computation.1 | async-start | bytes 6291456 | tf_op jit(solution)/shard_map/all_to_all | solution.py:137
  244.9 262.4 %copy-start.46 = (f32[384]{0:T(512)}, f32[384]{0:T(512)S(1)}, u32[]{:S(2)}) copy-start(f32[384]{0:T(512)S(1)} %mul.1143) | copy-start | bytes 4612
  307.2 636.9 %copy-start = (f32[1,2048,6,1,64]{1,4,3,2,0:T(8,128)}, f32[1,2048,6,1,64]{1,4,3,2,0:T(8,128)S(1)}, u32[]{:S(2)}) copy-start(f32[1,2048,6,1,64]{1,4,3,2,0:T(8,128)S(1)} %get-tuple-element.912) | copy-start | bytes 9437188
  559.7 25.3 %all-to-all-start.2 = ((bf16[8,2,49152]{2,1,0:T(2,128)(2,1)}), bf16[8,2,49152]{2,1,0:T(2,128)(2,1)}, u32[]{:S(2)}, u32[]{:S(2)}) async-start(bf16[8,2,49152]{2,1,0:T(2,128)(2,1)} %reshape.1695), calls=%async_computation.2 | async-start | bytes 3145728 | tf_op jit(solution)/shard_map/all_to_all | solution.py:154
  564.1 251.1 %reduce-scatter.8.cloned.1.call-start = ((), (), s32[]{:S(2)}) async-start(), calls=%async_computation.14 | async-start | bytes 19464192 | tf_op jit(solution)/shard_map/reduce_scatter | solution.py:222
  595.9 311.8 %copy-start.60 = (f32[256]{0:T(256)}, f32[256]{0:T(256)S(1)}, u32[]{:S(2)}) copy-start(f32[256]{0:T(256)S(1)} %get-tuple-element.936) | copy-start | bytes 3076
  610.9 288.4 %all-gather.8.cloned.1.call-start = ((), (), s32[]{:S(2)}) async-start(), calls=%async_computation.11 | async-start | bytes 9732096 | tf_op jit(solution)/shard_map/all_gather | solution.py:163
  939.1 25.3 %all-to-all-start.3 = ((bf16[8,2,49152]{2,1,0:T(2,128)(2,1)}), bf16[8,2,49152]{2,1,0:T(2,128)(2,1)}, u32[]{:S(2)}, u32[]{:S(2)}) async-start(bf16[8,2,49152]{2,1,0:T(2,128)(2,1)} %reshape.1697), calls=%async_computation.3 | async-start | bytes 3145728 | tf_op jit(solution)/shard_map/all_to_all | solution.py:178
  1354.7 88.3 %all-to-all-start.5 = ((bf16[8,2,768]{2,1,0:T(2,128)(2,1)}), bf16[8,2,768]{2,1,0:T(2,128)(2,1)S(1)}, u32[]{:S(2)}, u32[]{:S(2)}) async-start(bf16[8,2,768]{2,1,0:T(2,128)(2,1)} %reshape.1699), calls=%async_computation.6 | async-start | bytes 49152 | tf_op jit(solution)/shard_map/all_to_all | solution.py:184
  1443.0 45.4 %all-to-all-start.4 = ((bf16[8,2,98304]{2,1,0:T(2,128)(2,1)}), bf16[8,2,98304]{2,1,0:T(2,128)(2,1)}, u32[]{:S(2)}, u32[]{:S(2)}) async-start(bf16[8,2,98304]{2,1,0:T(2,128)(2,1)} %reshape.1701), calls=%async_computation.4 | async-start | bytes 6291456 | tf_op jit(solution)/shard_map/all_to_all | solution.py:183
  1447.7 54.6 %reduce-scatter.4.cloned.1.call-start = ((), (), s32[]{:S(2)}) async-start(), calls=%async_computation.12 | async-start | bytes 1179648 | tf_op jit(solution)/shard_map/reduce_scatter | solution.py:186
  1455.5 184.0 %all-reduce.32.cloned.1.call-start = ((), (), s32[]{:S(2)}) async-start(), calls=%async_computation.15 | async-start | bytes 258048 | tf_op jit(solution)/shard_map/psum | solution.py:209
  1514.9 494.2 %reduce-scatter.6.cloned.1.call-start = ((), (), s32[]{:S(2)}) async-start(), calls=%async_computation.13 | async-start | bytes 41361408 | tf_op jit(solution)/shard_map/reduce_scatter | solution.py:213
  1543.4 465.7 %copy-start.13 = (f32[48,6448]{1,0:T(8,128)S(1)}, f32[48,6448]{1,0:T(8,128)}, u32[]{:S(2)}) copy-start(f32[48,6448]{1,0:T(8,128)} %param.29) | copy-start | bytes 3714052
  1543.4 465.7 %copy-start.18 = (f32[48,6448]{1,0:T(8,128)S(1)}, f32[48,6448]{1,0:T(8,128)}, u32[]{:S(2)}) copy-start(f32[48,6448]{1,0:T(8,128)} %param.36) | copy-start | bytes 3714052
  1647.4 365.9 %copy-start.35 = (f32[1536]{0:T(1024)S(1)}, f32[1536]{0:T(1024)}, u32[]{:S(2)}) copy-start(f32[1536]{0:T(1024)} %get-tuple-element.1242) | copy-start | bytes 18436
  1647.4 366.5 %copy-start.33 = (f32[3072]{0:T(1024)S(1)}, f32[3072]{0:T(1024)}, u32[]{:S(2)}) copy-start(f32[3072]{0:T(1024)} %get-tuple-element.1243) | copy-start | bytes 36868
  1647.4 367.1 %copy-start.21 = (f32[5,3072]{1,0:T(8,128)S(1)}, f32[5,3072]{1,0:T(8,128)}, u32[]{:S(2)}) copy-start(f32[5,3072]{1,0:T(8,128)} %get-tuple-element.1244) | copy-start | bytes 184324
  1647.4 367.8 %copy-start.34 = (f32[5,256]{1,0:T(8,128)S(1)}, f32[5,256]{1,0:T(8,128)}, u32[]{:S(2)}) copy-start(f32[5,256]{1,0:T(8,128)} %get-tuple-element.1245) | copy-start | bytes 15364
  1647.4 368.4 %copy-start.73 = (f32[3,48]{1,0:T(4,128)S(1)}, f32[3,48]{1,0:T(4,128)}, u32[]{:S(2)}) copy-start(f32[3,48]{1,0:T(4,128)} %get-tuple-element.1246) | copy-start | bytes 1732
  (96 other events, 2495.9 us)
Sparse Core Ops, SparseCore 0:
  11.4 132.1 all-gather.3
  159.4 21.6 all-gather.5
  611.0 204.1 reduce-scatter.7
  818.7 80.5 all-gather.7
  1455.6 38.7 reduce-scatter.3
  1515.0 124.3 all-reduce.31
  1646.4 362.6 reduce-scatter.5
where the time goes:
time: 2040 us; the launch traced here: 2020 us
  waiting for transfers between devices  958 us (47%)
  local copies, waits for them, and re-layouts  484 us (24%)
  other arithmetic  326 us (16%)
  matrix products  211 us (10%)
  starting transfers between devices  25.1 us (1%)
    reduce_scatter x1, waiting for transfers between devices, local(): lax.psum_scatter(jnp.einsum('nkm,nkc->mc', column_list, projected_gradien...  362 us
    dynamic_update_slice x56, local copies, waits for them, and re-layouts, state_space(): lax.scan(jax.checkpoint(block_step), start, (blockify(inner), blockify(st...  215 us
    reduce_scatter x1, waiting for transfers between devices, local(): lax.psum_scatter(jnp.einsum('kcb,kch->bh', column_list, cotangent, prefer...  204 us
    all_gather x1, waiting for transfers between devices, local(): lax.all_gather(in_w16, ('seq', 'wshard'), axis=0, tiled=True)  132 us
    unnamed x10, other arithmetic  132 us
    psum x1, waiting for transfers between devices, local(): lax.psum((d_in_gain, d_out_gain, d_conv_full, d_common, d_head_full), ('s...  94.3 us
    another operation x49, other arithmetic  93.2 us
    all_gather x1, waiting for transfers between devices, local(): lax.all_gather(out_w16, ('seq', 'wshard'), axis=0, tiled=True)  76.8 us
  transfers between devices with their start and end apart: 13, of which 9 were waited for; matrix products, arithmetic and copies ran while one was open for 12% of the time, Pallas kernels for 0%

commit v1 on v0

--- a/solution.py
+++ b/solution.py
@@ -15,6 +15,18 @@
 weight_learning_rate = 0.01
 matrix_decay = 0.1
 small_rate = 0.1
+
+
+def doubled_up(x, axis, dim):
+    ways, here, lap = (lax.axis_size(axis), lax.axis_index(axis), x.shape[dim])
+    line, have = (x, 1)
+    while have < ways:
+        line = jnp.concatenate(
+            [line, lax.ppermute(line, axis, [(d, (d - have) % ways) for d in range(ways)])],
+            axis=dim,
+        )
+        have = 2 * have
+    return jnp.roll(line, here * lap, axis=dim)
 
 
 def causal_conv(values, taps):
@@ -127,7 +139,7 @@
     projected = jnp.einsum(
         "fbe,ek->fbk",
         column_list,
-        lax.all_gather(in_w16, ("seq", "wshard"), axis=0, tiled=True),
+        doubled_up(in_w16, ("seq", "wshard"), 0),
         preferred_element_type=jnp.float32,
     ).astype(jnp.bfloat16)
     gate_inner = projected[:, :, : 2 * E]

time: 2040 us -> 2520 us (1.24)
  waiting for transfers between devices: 958 us -> 1240 us
  local copies, waits for them, and re-layouts: 484 us -> 609 us
  matrix products: 211 us -> 252 us
    ppermute x0 -> x5, waiting for transfers between devices: none -> 407 us  [doubled_up(): lax.ppermute(line, axis, [(d, (d - have) % ways) for d in range(ways)])]
    all_gather x1, waiting for transfers between devices: 132 us -> 0.01 us  [local(): lax.all_gather(in_w16, ('seq', 'wshard'), axis=0, tiled=True)]
    concatenate x0 -> x3, local copies, waits for them, and re-layouts: none -> 90.1 us  [the longest x1 64.8 us: doubled_up(): return jnp.roll(line, here * lap, axis=dim)]
    unnamed x177 -> x183, local copies, waits for them, and re-layouts: 69 us -> 73.8 us
  transfers between devices with their start and end apart: 13 -> 18, of which waited for: 9 -> 13; matrix products, arithmetic and copies ran while one was open for 12% -> 29% of each run, Pallas kernels for 0% -> 0%
where the time goes in v1:
time: 2520 us; the launch traced here: 2500 us
  waiting for transfers between devices  1240 us (49%)
  local copies, waits for them, and re-layouts  609 us (24%)
  other arithmetic  344 us (14%)
  matrix products  252 us (10%)
  starting transfers between devices  39 us (2%)
    ppermute x5, waiting for transfers between devices, doubled_up(): lax.ppermute(line, axis, [(d, (d - have) % ways) for d in range(ways)])  407 us
    reduce_scatter x1, waiting for transfers between devices, local(): lax.psum_scatter(jnp.einsum('nkm,nkc->mc', column_list, projected_gradien...  362 us
    dynamic_update_slice x56, local copies, waits for them, and re-layouts, state_space(): lax.scan(jax.checkpoint(block_step), start, (blockify(inner), blockify(st...  215 us
    reduce_scatter x1, waiting for transfers between devices, local(): lax.psum_scatter(jnp.einsum('kcb,kch->bh', column_list, cotangent, prefer...  205 us
    unnamed x10, other arithmetic  133 us
    psum x1, waiting for transfers between devices, local(): lax.psum((d_in_gain, d_out_gain, d_conv_full, d_common, d_head_full), ('s...  94.2 us
    another operation x49, other arithmetic  93.2 us
    dot_general x24, matrix products, block_step(): within = jnp.einsum('sijh,sjhp->sihp', weights, inner_part, precision=high)  83.5 us
  transfers between devices with their start and end apart: 18, of which 13 were waited for; matrix products, arithmetic and copies ran while one was open for 29% of the time, Pallas kernels for 0%

profile of v1, /device:TPU:0, one launch (start us, length us, event | category | flops | bytes accessed | tf_op | source)
XLA Modules:
  0.0 2500.8 jit_solution(2325882373690745529)
XLA Ops:
  29.2 54.1 %collective-permute-done.1 = bf16[96,6448]{1,0:T(8,128)(2,1)S(1)} collective-permute-done((bf16[96,6448]{1,0:T(8,128)(2,1)S(1)}, bf16[96,6448]{1,0:T(8,128)(2,1)S(1)}, u32[]{:S(2)}, u32[]{:S(2)}) %collective-permute-start.1) | collective-permute-done | bytes 1238048 | tf_op jit(solution)/shard_map/ppermute | solution.py:25
  86.8 27.9 %collective-permute-done.2 = bf16[192,6448]{1,0:T(8,128)(2,1)S(1)} collective-permute-done((bf16[192,6448]{1,0:T(8,128)(2,1)S(1)}, bf16[192,6448]{1,0:T(8,128)(2,1)S(1)}, u32[]{:S(2)}, u32[]{:S(2)}) %collective-permute-start.2) | collective-permute-done | bytes 2476064 | tf_op jit(solution)/shard_map/ppermute | solution.py:25
  136.6 99.7 %collective-permute-done.3 = bf16[384,6448]{0,1:T(8,128)(2,1)} collective-permute-done((bf16[384,6448]{0,1:T(8,128)(2,1)}, bf16[384,6448]{0,1:T(8,128)(2,1)}, u32[]{:S(2)}, u32[]{:S(2)}) %collective-permute-start.3) | collective-permute-done | bytes 4952096 | tf_op jit(solution)/shard_map/ppermute | solution.py:25
  236.3 17.7 concatenate.28
  256.3 212.4 %collective-permute-done.4 = bf16[768,6448]{0,1:T(8,128)(2,1)} collective-permute-done((bf16[768,6448]{0,1:T(8,128)(2,1)}, bf16[768,6448]{0,1:T(8,128)(2,1)}, u32[]{:S(2)}, u32[]{:S(2)}) %collective-permute-start.4) | collective-permute-done | bytes 9904160 | tf_op jit(solution)/shard_map/ppermute | solution.py:25
  468.8 64.8 %concatenate.29 = bf16[3072,6448]{0,1:T(8,128)(2,1)} concatenate(bf16[48,6448]{0,1:T(8,128)(2,1)} %copy.525, bf16[48,6448]{0,1:T(8,128)(2,1)} %copy.526, bf16[96,6448]{0,1:T(8,128)(2,1)} %copy.527, bf16[192,6448]{0,1:T(8,128)(2,1)S(1)} %copy.528, bf16[384,6448]{0,1:T(8,128)(2,1)} %collective-permute-done.3, bf16[768,6448]{0,1:T(8,128)(2,1)} %collective-permute-done.4, ...), dimensions={0} | concatenate | bytes 79233024 | tf_op jit(solution)/shard_map/jit(_roll_dynamic)/concatenate | solution.py:29
  533.6 14.1 fusion.112
  555.2 37.2 %copy.667 = bf16[1,256,6144]{1,0,2:T(2,128)(2,1)} copy(bf16[1,256,6144]{1,2,0:T(8,128)(2,1)S(1)} %slice.200) | data formatting | bytes 6291456 | tf_op jit(solution)/shard_map/slice | solution.py:145
  592.4 31.5 %reduce.89 = bf16[6144,256]{1,0:T(8,128)(2,1)S(1)} reduce(bf16[6144,1,256]{2,1,0:T(2,128)(2,1)} %bitcast.656, bf16[]{:T(256)} %broadcast.1020), dimensions={1}, to_apply=%bitcast.469.reduce_sub_computation | reduce | bytes 6291458
  646.8 23.1 all-to-all-done.1
  705.3 192.1 %while.44 = (s32[]{:T(128)}, f32[1,6,64,128]{3,2,1,0:T(8,128)S(1)}, f32[8,1,256,6,64]{2,0,4,3,1:T(8,128)}, f32[8,1,6,64,128]{4,3,2,1,0:T(8,128)}, f32[8,1,256,6]...) while((s32[]{:T(128)}, f32[1,6,64,128]{3,2,1,0:T(8,128)S(1)}, ...), condition=%wide.region_4.5_spmd.clone.clone, body=%wide.region_1.4_spmd.clone.clone.sunk | while | flops 707349504 | bytes 5806421 | solution.py:71
  915.2 35.4 %reduce.90 = bf16[2048,384]{1,0:T(8,128)(2,1)} reduce(bf16[2048,1,384]{2,1,0:T(2,128)(2,1)} %bitcast.668, bf16[]{:T(256)} %broadcast.1020), dimensions={1}, to_apply=%bitcast.432.reduce_sub_computation | reduce | bytes 3145730
  958.7 20.9 all-to-all-done.2
  1005.5 205.4 %reduce-scatter.8.cloned.1.call-done = f32[96,1536]{1,0:T(8,128)} async-done(((f32[3072,1536]{1,0:T(8,128)}), f32[96,1536]{1,0:T(8,128)}) %reduce-scatter.8.cloned.1.call-update) | async-done | bytes 589840 | tf_op jit(solution)/shard_map/reduce_scatter | solution.py:234
  1218.2 76.9 %all-gather.6.cloned.1.call-done = bf16[3072,1536]{1,0:T(8,128)(2,1)} async-done(((bf16[96,1536]{1,0:T(8,128)(2,1)}), bf16[3072,1536]{1,0:T(8,128)(2,1)}) %all-gather.6.cloned.1.call-update) | async-done | bytes 9437200 | tf_op jit(solution)/shard_map/all_gather | solution.py:175
  1313.5 17.7 reduce.91
  1343.6 21.1 all-to-all-done.3
  1383.9 433.3 %while.43 = (s32[]{:T(128)}, f32[1,6,64,128]{3,2,1,0:T(8,128)S(1)}, f32[8,1,256,6,64]{2,0,4,3,1:T(8,128)}, f32[8,1,256,6]{3,2,1,0:T(8,128)}, f32[8,1,256,6]{2,0,...) while((s32[]{:T(128)}, f32[1,6,64,128]{3,2,1,0:T(8,128)S(1)}, ...), condition=%wide.region_19.20_spmd.clone, body=%wide.region_7.19_spmd.clone.sunk | while | flops 1670419456 | bytes 15190127 | solution.py:71
  1833.3 13.3 reduce.92
  1880.2 31.6 %reduce.93 = bf16[2048,768]{1,0:T(8,128)(2,1)S(1)} reduce(bf16[2048,1,768]{2,1,0:T(2,128)(2,1)} %bitcast.655, bf16[]{:T(256)} %broadcast.1020), dimensions={1}, to_apply=%bitcast.438.reduce_sub_computation | reduce | bytes 6291458
  1937.9 27.8 %all-to-all-done.4 = bf16[8,2,98304]{2,1,0:T(2,128)(2,1)} async-done(((bf16[8,2,98304]{2,1,0:T(2,128)(2,1)}), bf16[8,2,98304]{2,1,0:T(2,128)(2,1)}, u32[]{:S(2)}, u32[]{:S(2)}) %all-to-all-start.4) | async-done | bytes 3145760 | tf_op jit(solution)/shard_map/all_to_all | solution.py:195
  1992.3 18.5 fusion.142
  2022.4 94.2 %all-reduce.32.cloned.1.call-done = (f32[1536]{0:T(1024)}, f32[3072]{0:T(1024)}, f32[5,3072]{1,0:T(8,128)}, f32[5,256]{1,0:T(8,128)}, f32[3,48]{1,0:T(4,128)}) async-done(((f32[1536]{0:T(1024)}, f32[3072]{0:T(1024)}, f32[5,3072]{1,0:T(8,128)}, f32[5,256]{1,0:T(8,128)}, f32[3,48]{1,0:T(4,128)}), (f32[1536]{0:T(1024)}, f32[3072]{0:T(1024)}, f32[5,3072]{1,0:T(8,128)}, f32[5,256]{1,0:T(8,128)}, ...) | async-done | bytes 85584 | tf_op jit(solution)/shard_map/psum | solution.py:221
  2124.7 361.7 %reduce-scatter.6.cloned.1.call-done = f32[48,6448]{1,0:T(8,128)} async-done(((f32[1536,6448]{1,0:T(8,128)}), f32[48,6448]{1,0:T(8,128)}) %reduce-scatter.6.cloned.1.call-update) | async-done | bytes 1238032 | tf_op jit(solution)/shard_map/reduce_scatter | solution.py:225
  (973 shorter events, 975.5 us)
Async XLA Ops:
  7.2 628.5 %all-gather.4.cloned.1.call-start = ((), (), s32[]{:S(2)}) async-start(), calls=%async_computation.9 | async-start | bytes 1179648 | tf_op jit(solution)/shard_map/all_gather | solution.py:152
  8.6 19.1 collective-permute-start
  27.8 55.5 %collective-permute-start.1 = (bf16[96,6448]{1,0:T(8,128)(2,1)S(1)}, bf16[96,6448]{1,0:T(8,128)(2,1)S(1)}, u32[]{:S(2)}, u32[]{:S(2)}) collective-permute-start(bf16[96,6448]{1,0:T(8,128)(2,1)S(1)} %pad_maximum_fusion.2), channel_id=1, source_target_pairs={{0,30},{1,31},{2,0},{3,1},{4,2},{5,3},{6,4},{7,5},{8,6},{9,7},{10,... | collective-permute-start | bytes 3714056 | tf_op jit(solution)/shard_map/ppermute | solution.py:25
  83.5 31.2 %collective-permute-start.2 = (bf16[192,6448]{1,0:T(8,128)(2,1)S(1)}, bf16[192,6448]{1,0:T(8,128)(2,1)S(1)}, u32[]{:S(2)}, u32[]{:S(2)}) collective-permute-start(bf16[192,6448]{1,0:T(8,128)(2,1)S(1)} %pad_maximum_fusion.1), channel_id=1, source_target_pairs={{0,28},{1,29},{2,30},{3,31},{4,0},{5,1},{6,2},{7,3},{8,4},{9,5},{1... | collective-permute-start | bytes 7428104 | tf_op jit(solution)/shard_map/ppermute | solution.py:25
  126.7 109.5 %collective-permute-start.3 = (bf16[384,6448]{0,1:T(8,128)(2,1)}, bf16[384,6448]{0,1:T(8,128)(2,1)}, u32[]{:S(2)}, u32[]{:S(2)}) collective-permute-start(bf16[384,6448]{0,1:T(8,128)(2,1)} %copy.520), channel_id=1, source_target_pairs={{0,24},{1,25},{2,26},{3,27},{4,28},{5,29},{6,30},{7,31},{8,0},{9,1... | collective-permute-start | bytes 14856200 | tf_op jit(solution)/shard_map/ppermute | solution.py:25
  254.0 214.8 %collective-permute-start.4 = (bf16[768,6448]{0,1:T(8,128)(2,1)}, bf16[768,6448]{0,1:T(8,128)(2,1)}, u32[]{:S(2)}, u32[]{:S(2)}) collective-permute-start(bf16[768,6448]{0,1:T(8,128)(2,1)} %concatenate.28), channel_id=1, source_target_pairs={{0,16},{1,17},{2,18},{3,19},{4,20},{5,21},{6,22},{7,23},{8,24},{9,... | collective-permute-start | bytes 29712392 | tf_op jit(solution)/shard_map/ppermute | solution.py:25
  550.4 77.2 %all-to-all-start = ((bf16[8,2,768]{2,1,0:T(2,128)(2,1)}), bf16[8,2,768]{2,1,0:T(2,128)(2,1)S(1)}, u32[]{:S(2)}, u32[]{:S(2)}) async-start(bf16[8,2,768]{2,1,0:T(2,128)(2,1)} %reshape.1691), calls=%async_computation | async-start | bytes 49152 | tf_op jit(solution)/shard_map/all_to_all | solution.py:150
  627.6 42.4 %all-to-all-start.1 = ((bf16[8,2,98304]{2,1,0:T(2,128)(2,1)}), bf16[8,2,98304]{2,1,0:T(2,128)(2,1)S(1)}, u32[]{:S(2)}, u32[]{:S(2)}) async-start(bf16[8,2,98304]{2,1,0:T(2,128)(2,1)} %reshape.1693), calls=%async_computation.1 | async-start | bytes 6291456 | tf_op jit(solution)/shard_map/all_to_all | solution.py:149
  634.1 705.7 %copy-start.19 = (bf16[48,1,256]{2,1,0:T(2,128)(2,1)}, bf16[48,1,256]{2,1,0:T(2,128)(2,1)S(1)}, u32[]{:S(2)}) copy-start(bf16[48,1,256]{2,1,0:T(2,128)(2,1)S(1)} %reshape.1692) | copy-start | bytes 73732
  694.7 645.8 %copy-start = (f32[1,2048,6,1,64]{1,4,3,2,0:T(8,128)}, f32[1,2048,6,1,64]{1,4,3,2,0:T(8,128)S(1)}, u32[]{:S(2)}) copy-start(f32[1,2048,6,1,64]{1,4,3,2,0:T(8,128)S(1)} %get-tuple-element.912) | copy-start | bytes 9437188
  954.3 25.3 %all-to-all-start.2 = ((bf16[8,2,49152]{2,1,0:T(2,128)(2,1)}), bf16[8,2,49152]{2,1,0:T(2,128)(2,1)}, u32[]{:S(2)}, u32[]{:S(2)}) async-start(bf16[8,2,49152]{2,1,0:T(2,128)(2,1)} %reshape.1695), calls=%async_computation.2 | async-start | bytes 3145728 | tf_op jit(solution)/shard_map/all_to_all | solution.py:166
  958.6 252.3 %reduce-scatter.8.cloned.1.call-start = ((), (), s32[]{:S(2)}) async-start(), calls=%async_computation.14 | async-start | bytes 19464192 | tf_op jit(solution)/shard_map/reduce_scatter | solution.py:234
  1005.5 289.7 %all-gather.6.cloned.1.call-start = ((), (), s32[]{:S(2)}) async-start(), calls=%async_computation.10 | async-start | bytes 9732096 | tf_op jit(solution)/shard_map/all_gather | solution.py:175
  1334.9 29.8 %all-to-all-start.3 = ((bf16[8,2,49152]{2,1,0:T(2,128)(2,1)}), bf16[8,2,49152]{2,1,0:T(2,128)(2,1)}, u32[]{:S(2)}, u32[]{:S(2)}) async-start(bf16[8,2,49152]{2,1,0:T(2,128)(2,1)} %reshape.1697), calls=%async_computation.3 | async-start | bytes 3145728 | tf_op jit(solution)/shard_map/all_to_all | solution.py:190
  1339.2 640.4 %all-gather.8.cloned.1.call-start = ((), (), s32[]{:S(2)}) async-start(), calls=%async_computation.12 | async-start | bytes 20680704 | tf_op jit(solution)/shard_map/all_gather | solution.py:205
  1849.1 71.2 %all-to-all-start.5 = ((bf16[8,2,768]{2,1,0:T(2,128)(2,1)}), bf16[8,2,768]{2,1,0:T(2,128)(2,1)S(1)}, u32[]{:S(2)}, u32[]{:S(2)}) async-start(bf16[8,2,768]{2,1,0:T(2,128)(2,1)} %reshape.1699), calls=%async_computation.6 | async-start | bytes 49152 | tf_op jit(solution)/shard_map/all_to_all | solution.py:196
  1920.2 45.4 %all-to-all-start.4 = ((bf16[8,2,98304]{2,1,0:T(2,128)(2,1)}), bf16[8,2,98304]{2,1,0:T(2,128)(2,1)}, u32[]{:S(2)}, u32[]{:S(2)}) async-start(bf16[8,2,98304]{2,1,0:T(2,128)(2,1)} %reshape.1701), calls=%async_computation.4 | async-start | bytes 6291456 | tf_op jit(solution)/shard_map/all_to_all | solution.py:195
  1925.0 54.7 %reduce-scatter.4.cloned.1.call-start = ((), (), s32[]{:S(2)}) async-start(), calls=%async_computation.11 | async-start | bytes 1179648 | tf_op jit(solution)/shard_map/reduce_scatter | solution.py:198
  1932.7 184.0 %all-reduce.32.cloned.1.call-start = ((), (), s32[]{:S(2)}) async-start(), calls=%async_computation.15 | async-start | bytes 258048 | tf_op jit(solution)/shard_map/psum | solution.py:221
  1992.2 494.1 %reduce-scatter.6.cloned.1.call-start = ((), (), s32[]{:S(2)}) async-start(), calls=%async_computation.13 | async-start | bytes 41361408 | tf_op jit(solution)/shard_map/reduce_scatter | solution.py:225
  2020.7 465.6 %copy-start.13 = (f32[48,6448]{1,0:T(8,128)S(1)}, f32[48,6448]{1,0:T(8,128)}, u32[]{:S(2)}) copy-start(f32[48,6448]{1,0:T(8,128)} %param.29) | copy-start | bytes 3714052
  2020.7 465.6 %copy-start.18 = (f32[48,6448]{1,0:T(8,128)S(1)}, f32[48,6448]{1,0:T(8,128)}, u32[]{:S(2)}) copy-start(f32[48,6448]{1,0:T(8,128)} %param.36) | copy-start | bytes 3714052
  2124.7 367.7 %copy-start.36 = (f32[5,256]{1,0:T(8,128)S(1)}, f32[5,256]{1,0:T(8,128)}, u32[]{:S(2)}) copy-start(f32[5,256]{1,0:T(8,128)} %get-tuple-element.1245) | copy-start | bytes 15364
  2124.7 368.3 %copy-start.75 = (f32[3,48]{1,0:T(4,128)S(1)}, f32[3,48]{1,0:T(4,128)}, u32[]{:S(2)}) copy-start(f32[3,48]{1,0:T(4,128)} %get-tuple-element.1246) | copy-start | bytes 1732
  (96 other events, 4346.8 us)
Sparse Core Ops, SparseCore 0:
  548.5 24.1 all-gather.3
  1005.6 205.2 reduce-scatter.7
  1214.5 80.6 all-gather.5
  1342.5 132.7 all-gather.7
  1932.8 38.7 reduce-scatter.3
  1992.3 124.2 all-reduce.31
  2123.6 362.6 reduce-scatter.5
